TPU v7x, 256 devices: a whole 4x4x8 slice. The times are simulated.
256 devices in a mesh: fit: 64 (over x, y_lo, z), col: 4 (over y_hi, core).
Axes of the slice: x: 4, y: 4 (y_hi: 2, y_lo: 2; y = y_hi * 2 + y_lo), z: 8, core: 2. Of those that a mesh axis runs over, the one named last changes fastest.
Arguments:
- trial: bfloat16 [8, 256, 512], P(None, 'fit', 'col'), may hold values from -6 to 6
- hole_factor: bfloat16 [2048, 256, 256], P('fit'), may hold values from -0.0234375 to 0.0234375
- elec_factor: bfloat16 [2048, 512, 512], P('fit', 'col'), may hold values from -0.25 to 0.25
- hole_energy: float32 [256], P('fit'), may hold values from -1.2 to -0.3
- elec_energy: float32 [512], P('col'), may hold values from 0.1 to 1.5
Outputs:
- applied: float32 [8, 256, 512], P(None, 'fit', 'col')
All inputs are finite; a program needn't handle non-finite values.
Results may differ from a plain program's by a relative error of at most 0.0018.
Values may be sent and summed in bfloat16 or wider, within the bound.
A program may use at most 64 MiB of HBM per device.

v0:
```python
import jax
import jax.numpy as jnp
from jax import lax
from jax.sharding import PartitionSpec as P


def in_order(blocks, dim):
    blocks = jnp.moveaxis(blocks, 0, dim)
    dims = blocks.shape
    return blocks.reshape(*dims[:dim], dims[dim] * dims[dim + 1], *dims[dim + 2 :])


def copy_for_each(array, axis):
    devices = lax.axis_size(axis)
    return lax.all_to_all(
        jnp.broadcast_to(array[None], (devices, *array.shape)), axis, 0, 0, tiled=True
    )


def gather_directly(array, axis, dim):
    return in_order(copy_for_each(array, axis), dim)


def in_blocks(array, dim, devices):
    before, after = (array.shape[:dim], array.shape[dim + 1 :])
    return jnp.moveaxis(array.reshape(*before, devices, -1, *after), dim, 0)


def summed_on_arrival(array, axis, dim):
    blocks = in_blocks(array, dim, lax.axis_size(axis))
    arrived = lax.all_to_all(blocks, axis, split_axis=0, concat_axis=0, tiled=True)
    return arrived.sum(axis=0)


def local(trial, hole_factor, elec_factor, hole_energy, elec_energy):
    wide_rows = gather_directly(trial, "col", 2)
    half = jnp.einsum(
        "krb,pab->kpra",
        lax.all_gather(wide_rows, "fit", axis=1, tiled=True),
        elec_factor,
        preferred_element_type=jnp.float32,
    ).astype(jnp.bfloat16)
    partial_value = jnp.einsum(
        "pij,kpja->kia", hole_factor, half, preferred_element_type=jnp.float32
    )
    direct = summed_on_arrival(partial_value, "fit", 1)
    spread = elec_energy[None, :] - hole_energy[:, None]
    return direct + spread[None] * trial.astype(jnp.float32)


def solution(mesh):
    in_specs = (
        P(None, "fit", "col"),
        P("fit", None, None),
        P("fit", "col", None),
        P("fit"),
        P("col"),
    )
    out_specs = P(None, "fit", "col")
    return jax.shard_map(local, mesh=mesh, in_specs=in_specs, out_specs=out_specs, check_vma=False)
```

profile of v0, /device:TPU:8, one launch (start us, length us, event | category | flops | bytes accessed | tf_op | source)
XLA Modules:
  0.0 377.7 jit_solution(14945522642771570225)
XLA Ops:
  6.5 0.0 all-gather.2.cloned.1.call-start
  6.5 0.7 copy.8
  7.2 8.8 %all_to_all.10 = bf16[4,8,4,128]{3,1,2,0:T(8,128)(2,1)S(1)} all-to-all(bf16[4,8,4,128]{3,1,2,0:T(8,128)(2,1)S(1)} %broadcast_in_dim.2), channel_id=1, replica_groups=mesh['fit'=64,'col'=4] {'col'}, dimensions={0} | all-to-all | bytes 65536 | tf_op jit(solution)/shard_map/all_to_all | solution.py:15
  16.1 0.6 copy_bitcast_fusion
  16.7 0.0 all-gather.2.cloned.1.call-update
  16.7 289.2 %all-gather.2.cloned.1.call-done = bf16[8,256,512]{2,0,1:T(8,128)(2,1)} async-done(((bf16[8,4,512]{2,0,1:T(8,128)(2,1)}), bf16[8,256,512]{2,0,1:T(8,128)(2,1)}) %all-gather.2.cloned.1.call-update) | async-done | bytes 2097168 | tf_op jit(solution)/shard_map/all_gather | solution.py:39
  305.9 24.8 %fusion.10 = f32[8,256,128]{1,2,0:T(8,128)S(1)} fusion(bf16[32,256,256]{2,1,0:T(8,128)(2,1)} %param.6, bf16[32,128,512]{2,1,0:T(8,128)(2,1)} %param.7, bf16[8,256,512,1]{2,0,1,3:T(8,128)(2,1)} %bitcast.31), kind=kOutput, calls=%fused_computation.7 | convolution fusion | flops 12893290496 | bytes 11534336 | tf_op jit(solution)/shard_map/pij,kpja->kia/dot_general | solution.py:43
  330.7 0.0 copy-start.1
  330.7 0.0 copy-start.2
  330.7 0.0 copy-start
  330.7 1.3 copy.11
  332.1 19.8 %all-to-all-start.1 = ((f32[64,8,4,128]{3,1,2,0:T(8,128)}), f32[64,8,4,128]{3,1,2,0:T(8,128)S(1)}, u32[]{:S(2)}, u32[]{:S(2)}) async-start(f32[64,8,4,128]{3,1,2,0:T(8,128)} %bitcast.9), calls=%async_computation.1 | async-start | bytes 2097152 | tf_op jit(solution)/shard_map/all_to_all | solution.py:31
  351.9 0.0 copy-done.1
  351.9 0.0 copy-done.2
  351.9 0.1 broadcast_subtract_fusion
  351.9 18.2 %all-to-all-done.1 = f32[64,8,4,128]{3,1,2,0:T(8,128)S(1)} async-done(((f32[64,8,4,128]{3,1,2,0:T(8,128)}), f32[64,8,4,128]{3,1,2,0:T(8,128)S(1)}, u32[]{:S(2)}, u32[]{:S(2)}) %all-to-all-start.1) | async-done | bytes 1048608 | tf_op jit(solution)/shard_map/all_to_all | solution.py:31
  370.1 0.1 reduce_sum.9
  370.2 0.0 copy-done
  370.2 0.6 copy.13
  (2 shorter events, 0.0 us)
Async XLA Ops:
  6.5 299.4 %all-gather.2.cloned.1.call-start = ((), (), s32[]{:S(2)}) async-start(), calls=%async_computation.2 | async-start | bytes 2129920 | tf_op jit(solution)/shard_map/all_gather | solution.py:39
  330.7 21.1 %copy-start.1 = (f32[4]{0:T(128)S(1)}, f32[4]{0:T(128)}, u32[]{:S(2)}) copy-start(f32[4]{0:T(128)} %param.8) | copy-start | bytes 52
  330.7 21.1 %copy-start.2 = (f32[128]{0:T(128)S(1)}, f32[128]{0:T(128)}, u32[]{:S(2)}) copy-start(f32[128]{0:T(128)} %param.9) | copy-start | bytes 1540
  330.7 39.5 %copy-start = (bf16[8,4,128]{2,1,0:T(4,128)(2,1)S(1)}, bf16[8,4,128]{2,1,0:T(4,128)(2,1)}, u32[]{:S(2)}) copy-start(bf16[8,4,128]{2,1,0:T(4,128)(2,1)} %param.5) | copy-start | bytes 24580
  332.1 38.0 %all-to-all-start.1 = ((f32[64,8,4,128]{3,1,2,0:T(8,128)}), f32[64,8,4,128]{3,1,2,0:T(8,128)S(1)}, u32[]{:S(2)}, u32[]{:S(2)}) async-start(f32[64,8,4,128]{3,1,2,0:T(8,128)} %bitcast.9), calls=%async_computation.1 | async-start | bytes 2097152 | tf_op jit(solution)/shard_map/all_to_all | solution.py:31
Sparse Core Ops, SparseCore 0:
  16.8 289.0 all-gather.1
where the time goes:
time: 379 us; the launch traced here: 378 us
  waiting for transfers between devices  307 us (81%)
  matrix products  24.8 us (7%)
  starting transfers between devices  19.8 us (5%)
  between operations  13.5 us (4%)
  blocking collectives  8.82 us (2%)
    all_gather x1, waiting for transfers between devices, local(): lax.all_gather(wide_rows, 'fit', axis=1, tiled=True)  289 us
    dot_general x1, matrix products, local(): jnp.einsum('pij,kpja->kia', hole_factor, half, preferred_element_type=jnp...  24.8 us
    all_to_all x1, starting transfers between devices, summed_on_arrival(): lax.all_to_all(blocks, axis, split_axis=0, concat_axis=0, tiled=True)  19.8 us
    all_to_all x1, waiting for transfers between devices, summed_on_arrival(): lax.all_to_all(blocks, axis, split_axis=0, concat_axis=0, tiled=True)  18.2 us
    all_to_all x1, blocking collectives, copy_for_each(): lax.all_to_all(jnp.broadcast_to(array[None], (devices, *array.shape)), ax...  8.82 us
  transfers between devices with their start and end apart: 2, of which 2 were waited for; matrix products, arithmetic and copies ran while one was open for 0% of the time, Pallas kernels for 0%

commit v1 on v0

v1 whole, which is shorter than its diff:
```python
import jax
import jax.numpy as jnp
from jax import lax
from jax.experimental import pallas as pl
from jax.experimental.pallas import tpu as pltpu
from jax.sharding import PartitionSpec as P

MESH = pl.DeviceIdType.MESH
F32, BF16 = jnp.float32, jnp.bfloat16

X, YH, YL, Z = 4, 2, 2, 8
NK, NO, NV = 8, 256, 512
CH = 4
KC = NK // CH
LINES = X * YL
ROWS = NO // LINES
OWN = NO // (LINES * Z)
AUX = 32
W = 128
MB = 2048


def nt(a, b):
    return lax.dot_general(a, b, (((1,), (1,)), ((), ())), preferred_element_type=F32)


def kernel(
    trial, hole_hbm, elec_hbm, out,
    elec, hole, hole_t, rz, line, full, half, acc, part, got, part2, got2,
    load_sem, zs, zr, ps, pr, cs, cr, s1, r1, s2, r2,
):
    f, c = lax.axis_index("fit"), lax.axis_index("col")
    x, yl, z = f // (YL * Z), (f // Z) % YL, f % Z
    yh, core = c // 2, c % 2
    ln = f // Z
    y = yh * YL + yl
    q = x * 4 + y

    def at_z(off):
        return (ln * Z + (z + off) % Z, c)

    def at_plane(off):
        q2 = (q + off) % 16
        x2, y2 = q2 // 4, q2 % 4
        return ((x2 * YL + y2 % YL) * Z + z, (y2 // YL) * 2 + core)

    def at_line(off):
        return (((ln + off) % LINES) * Z + z, c)

    partner = (f, yh * 2 + (1 - core))

    def load_hole():
        return pltpu.make_async_copy(hole_hbm, hole, load_sem.at[0])

    def load_elec():
        return pltpu.make_async_copy(elec_hbm, elec, load_sem.at[1])

    load_hole().start()
    load_elec().start()

    barrier = pltpu.get_barrier_semaphore()

    @pl.loop(1, Z)
    def _(off):
        pl.semaphore_signal(barrier, inc=1, device_id=at_z(off), device_id_type=MESH)

    @pl.loop(1, 16)
    def _(off):
        pl.semaphore_signal(barrier, inc=1, device_id=at_plane(off), device_id_type=MESH)

    pl.semaphore_signal(barrier, inc=1, device_id=partner, device_id_type=MESH)
    pl.semaphore_wait(barrier, Z - 1 + 15 + 1)

    def z_copy(off):
        return pltpu.make_async_remote_copy(
            src_ref=trial, dst_ref=rz.at[z], send_sem=zs.at[off], recv_sem=zr.at[off],
            device_id=at_z(off), device_id_type=MESH,
        )

    @pl.loop(1, Z)
    def _(off):
        z_copy(off).start()

    rz[z] = trial[...]
    load_hole().wait()

    @pl.loop(0, AUX)
    def _(p):
        hole_t[pl.ds(pl.multiple_of(p * NO, NO), NO), :] = hole[p].T

    @pl.loop(1, Z)
    def _(off):
        z_copy(off).wait_recv()

    for zz in range(Z):
        for k in range(NK):
            line[k, zz * OWN : (zz + 1) * OWN, :] = rz[zz, k].astype(F32)
    mine = pl.ds(pl.multiple_of(ln * ROWS, ROWS), ROWS)
    full[c, :, mine, :] = line[...].astype(BF16)

    def plane_copy(ch, off):
        here = full.at[c, pl.ds(ch * KC, KC), mine, :]
        return pltpu.make_async_remote_copy(
            src_ref=here, dst_ref=here, send_sem=ps.at[ch, off], recv_sem=pr.at[ch, off],
            device_id=at_plane(off), device_id_type=MESH,
        )

    for ch in range(CH):
        @pl.loop(1, 16)
        def _(off):
            plane_copy(ch, off).start()

    def core_copy(ch, h):
        here = full.at[2 * h + core, pl.ds(ch * KC, KC)]
        return pltpu.make_async_remote_copy(
            src_ref=here, dst_ref=here, send_sem=cs.at[ch, h], recv_sem=cr.at[ch, h],
            device_id=partner, device_id_type=MESH,
        )

    def hand_over(ch):
        @pl.loop(1, 16)
        def _(off):
            plane_copy(ch, off).wait_recv()

        for h in range(2):
            core_copy(ch, h).start()

    def sum_copy(ch, off):
        there = (ln + off) % LINES
        return pltpu.make_async_remote_copy(
            src_ref=part.at[ch, pl.ds(pl.multiple_of(there * ROWS, ROWS), ROWS), :],
            dst_ref=got.at[ch, ln], send_sem=s1.at[ch, off], recv_sem=r1.at[ch, off],
            device_id=at_line(off), device_id_type=MESH,
        )

    def sum2_copy(ch, off):
        return pltpu.make_async_remote_copy(
            src_ref=part2.at[ch, (z + off) % Z], dst_ref=got2.at[ch, z],
            send_sem=s2.at[ch, off], recv_sem=r2.at[ch, off],
            device_id=at_z(off), device_id_type=MESH,
        )

    def first_sum(ch):
        @pl.loop(1, LINES)
        def _(off):
            sum_copy(ch, off).wait_recv()

        total = got[ch, 0].astype(F32)
        for n in range(1, LINES):
            total = total + got[ch, n].astype(F32)
        for zz in range(Z):
            part2[ch, zz] = total[zz * OWN : (zz + 1) * OWN, :]
        got2[ch, z] = part2[ch, z]

        @pl.loop(1, Z)
        def _(off):
            sum2_copy(ch, off).start()

    def second_sum(ch):
        @pl.loop(1, Z)
        def _(off):
            sum2_copy(ch, off).wait_recv()

        total = got2[ch, 0]
        for n in range(1, Z):
            total = total + got2[ch, n]
        for kk in range(KC):
            out[ch * KC + kk] = total[:, kk * W : (kk + 1) * W]

    load_elec().wait()
    hand_over(0)
    for ch in range(CH):
        for h in range(2):
            core_copy(ch, h).wait_recv()

        for kk in range(KC):
            @pl.loop(0, AUX * W // MB)
            def _(m):
                left = elec[pl.ds(pl.multiple_of(m * MB, MB), MB), :]
                right = jnp.concatenate([full[b, ch * KC + kk] for b in range(4)], axis=1)
                made = nt(left, right)
                for p in range(MB // W):
                    at = pl.multiple_of(m * (MB // W * NO) + p * NO, NO)
                    half[kk * W : (kk + 1) * W, pl.ds(at, NO)] = made[p * W : (p + 1) * W].astype(BF16)

        if ch + 1 < CH:
            hand_over(ch + 1)
        if ch >= 1:
            first_sum(ch - 1)

        acc[...] = jnp.dot(half[...], hole_t[...], preferred_element_type=F32)
        part[ch] = acc[...].T.astype(BF16)
        got[ch, ln] = part[ch, mine, :]

        @pl.loop(1, LINES)
        def _(off):
            sum_copy(ch, off).start()

        if ch >= 2:
            second_sum(ch - 2)

    first_sum(CH - 1)
    second_sum(CH - 2)
    second_sum(CH - 1)

    @pl.loop(1, Z)
    def _(off):
        z_copy(off).wait_send()

    for ch in range(CH):
        @pl.loop(1, 16)
        def _(off):
            plane_copy(ch, off).wait_send()

        for h in range(2):
            core_copy(ch, h).wait_send()

        @pl.loop(1, LINES)
        def _(off):
            sum_copy(ch, off).wait_send()

        @pl.loop(1, Z)
        def _(off):
            sum2_copy(ch, off).wait_send()


def local(trial, hole_factor, elec_factor, hole_energy, elec_energy):
    vmem, hbm = pl.BlockSpec(memory_space=pltpu.VMEM), pl.BlockSpec(memory_space=pl.ANY)
    dma = pltpu.SemaphoreType.DMA
    direct = pl.pallas_call(
        kernel,
        out_shape=jax.ShapeDtypeStruct((NK, OWN, W), F32),
        in_specs=[vmem, hbm, hbm],
        out_specs=vmem,
        scratch_shapes=[
            pltpu.VMEM((AUX * W, NV), BF16),
            pltpu.VMEM((AUX, NO, NO), BF16),
            pltpu.VMEM((AUX * NO, NO), BF16),
            pltpu.VMEM((Z, NK, OWN, W), BF16),
            pltpu.VMEM((NK, ROWS, W), F32),
            pltpu.VMEM((4, NK, NO, W), BF16),
            pltpu.VMEM((KC * W, AUX * NO), BF16),
            pltpu.VMEM((KC * W, NO), F32),
            pltpu.VMEM((CH, NO, KC * W), BF16),
            pltpu.VMEM((CH, LINES, ROWS, KC * W), BF16),
            pltpu.VMEM((CH, Z, OWN, KC * W), F32),
            pltpu.VMEM((CH, Z, OWN, KC * W), F32),
            dma((2,)),
            dma((Z,)), dma((Z,)),
            dma((CH, 16)), dma((CH, 16)),
            dma((CH, 2)), dma((CH, 2)),
            dma((CH, LINES)), dma((CH, LINES)),
            dma((CH, Z)), dma((CH, Z)),
        ],
        compiler_params=pltpu.CompilerParams(
            collective_id=0, has_side_effects=True, vmem_limit_bytes=60 * 1024 * 1024
        ),
        name="bse_direct",
    )(trial, hole_factor, elec_factor.reshape(AUX * W, NV))
    spread = elec_energy[None, :] - hole_energy[:, None]
    return direct + spread[None] * trial.astype(F32)


def solution(mesh):
    in_specs = (
        P(None, "fit", "col"),
        P("fit", None, None),
        P("fit", "col", None),
        P("fit"),
        P("col"),
    )
    out_specs = P(None, "fit", "col")
    return jax.shard_map(local, mesh=mesh, in_specs=in_specs, out_specs=out_specs, check_vma=False)
```

time: 379 us -> 62.1 us (0.16)
  waiting for transfers between devices: 307 us -> 0 us
  Pallas kernels: 0 us -> 59.7 us
  matrix products: 24.8 us -> 0 us
  starting transfers between devices: 19.8 us -> 0 us
  between operations: 13.5 us -> 0.02 us
  blocking collectives: 8.82 us -> 0 us
    all_gather x1 -> x0, waiting for transfers between devices: 289 us -> none  [local(): lax.all_gather(wide_rows, 'fit', axis=1, tiled=True)]
    pallas_call x0 -> x1, Pallas kernels: none -> 59.7 us  [local(): pl.pallas_call(kernel, out_shape=jax.ShapeDtypeStruct((NK, OWN, W), F32),...]
    dot_general x1 -> x0, matrix products: 24.8 us -> none  [local(): jnp.einsum('pij,kpja->kia', hole_factor, half, preferred_element_type=jnp...]
    all_to_all x1 -> x0, starting transfers between devices: 19.8 us -> none  [summed_on_arrival(): lax.all_to_all(blocks, axis, split_axis=0, concat_axis=0, tiled=True)]
    all_to_all x1 -> x0, waiting for transfers between devices: 18.2 us -> none  [summed_on_arrival(): lax.all_to_all(blocks, axis, split_axis=0, concat_axis=0, tiled=True)]
    all_to_all x1 -> x0, blocking collectives: 8.82 us -> none  [copy_for_each(): lax.all_to_all(jnp.broadcast_to(array[None], (devices, *array.shape)), ax...]
  transfers between devices with their start and end apart: 2 -> 0, of which waited for: 2 -> 0; matrix products, arithmetic and copies ran while one was open for 0% -> 0% of each run, Pallas kernels for 0% -> 0%
where the time goes in v1:
time: 62.1 us; the launch traced here: 61.8 us
  Pallas kernels  59.7 us (96%)
  other arithmetic  2.07 us (3%)
    pallas_call x1, Pallas kernels, local(): pl.pallas_call(kernel, out_shape=jax.ShapeDtypeStruct((NK, OWN, W), F32),...  59.7 us
    add x1, other arithmetic, local(): return direct + spread[None] * trial.astype(F32)  1.33 us

profile of v1, /device:TPU:8, one launch (start us, length us, event | category | flops | bytes accessed | tf_op | source)
XLA Modules:
  0.0 61.8 jit_solution(362213683738318487)
XLA Ops:
  0.0 0.7 %broadcast_subtract_fusion = f32[4,128]{1,0:T(4,128)S(1)} fusion(f32[4]{0:T(128)} %param.8, f32[128]{0:T(128)} %param.9), kind=kLoop, calls=%fused_computation.1 | loop fusion | flops 512 | bytes 2576 | tf_op jit(solution)/shard_map/sub | solution.py:260
  0.7 0.0 copy-start
  0.7 59.7 %bse_direct.1 = f32[8,4,128]{2,1,0:T(4,128)} custom-call(bf16[8,4,128]{2,1,0:T(4,128)(2,1)} %trial.1, bf16[32,256,256]{2,1,0:T(8,128)(2,1)} %hole_hbm.1, bf16[4096,512]{1,0:T(8,128)(2,1)} %bitcast.5), custom_call_target="tpu_custom_call" | custom-call | tf_op jit(solution)/shard_map/bse_direct/pallas_call | solution.py:230
  60.5 0.0 copy-done
  60.5 1.3 %multiply_add_fusion = f32[4,8,128]{2,1,0:T(8,128)} fusion(f32[4,8,128]{2,1,0:T(8,128)} %bitcast.6, bf16[4,8,128]{2,1,0:T(8,128)(2,1)S(1)} %bitcast.7, f32[8,128]{1,0:T(8,128)S(1)} %bitcast.8), kind=kLoop, calls=%fused_computation | loop fusion | flops 12288 | bytes 45056 | tf_op jit(solution)/shard_map/add | solution.py:261
  (1 shorter events, 0.0 us)
Async XLA Ops:
  0.7 59.7 %copy-start = (bf16[8,4,128]{2,1,0:T(4,128)(2,1)S(1)}, bf16[8,4,128]{2,1,0:T(4,128)(2,1)}, u32[]{:S(2)}) copy-start(bf16[8,4,128]{2,1,0:T(4,128)(2,1)} %trial.1) | copy-start | bytes 24580

commit v2 on v0

v2 whole, which is shorter than its diff:
```python
import jax
import jax.numpy as jnp
from jax import lax
from jax.experimental import pallas as pl
from jax.experimental.pallas import tpu as pltpu
from jax.sharding import PartitionSpec as P

MESH = pl.DeviceIdType.MESH
F32, BF16 = jnp.float32, jnp.bfloat16

X, YH, YL, Z = 4, 2, 2, 8
PLANE = X * YH * YL
NK, NO, NV = 8, 256, 512
CH = 4
KC = NK // CH
LINES = X * YL
ROWS = NO // LINES
OWN = NO // (LINES * Z)
AUX = 32
W = 128
MB = 2048
LAG, LAG2 = 2, 4


def nt(a, b):
    return lax.dot_general(a, b, (((1,), (1,)), ((), ())), preferred_element_type=F32)


def kernel(
    trial, hole_hbm, elec_hbm, hole_e, elec_e, out,
    elec, hole, hole_t, rz, line, full, half, acc, part, got, part2, got2,
    load_sem, zs, zr, ps, pr, cs, cr, s1, r1, s2, r2,
):
    f, c = lax.axis_index("fit"), lax.axis_index("col")
    ln, z = lax.div(f, Z), lax.rem(f, Z)
    x, yl = lax.div(ln, YL), lax.rem(ln, YL)
    yh, core = lax.div(c, 2), lax.rem(c, 2)
    q = x * 4 + yh * YL + yl

    def plane_of(off):
        q2 = lax.rem(q + off, PLANE)
        x2, y2 = lax.div(q2, 4), lax.rem(q2, 4)
        return (x2 * YL + lax.rem(y2, YL)) * Z + z, lax.div(y2, YL) * 2 + core

    z_at = [lax.rem(z + o, Z) for o in range(Z)]
    line_at = [lax.rem(ln + o, LINES) for o in range(LINES)]
    z_peer = [(ln * Z + z_at[o], c) for o in range(Z)]
    line_peer = [(line_at[o] * Z + z, c) for o in range(LINES)]
    plane_peer = [plane_of(o) for o in range(PLANE)]
    partner = (f, yh * 2 + (1 - core))
    mine = pl.ds(pl.multiple_of(ln * ROWS, ROWS), ROWS)

    def load(n, src, dst):
        return pltpu.make_async_copy(src, dst, load_sem.at[n])

    load_trial = load(0, trial, rz.at[z])
    load_hole = load(1, hole_hbm, hole)
    load_elec = load(2, elec_hbm, elec)
    load_trial.start()

    barrier = pltpu.get_barrier_semaphore()
    for peer in z_peer[1:] + plane_peer[1:] + [partner]:
        pl.semaphore_signal(barrier, inc=1, device_id=peer, device_id_type=MESH)
    load_hole.start()
    load_elec.start()
    load_trial.wait()
    pl.semaphore_wait(barrier, Z - 1 + PLANE - 1 + 1)

    def remote(src, dst, send, recv, peer):
        return pltpu.make_async_remote_copy(
            src_ref=src, dst_ref=dst, send_sem=send, recv_sem=recv, device_id=peer, device_id_type=MESH
        )

    def arrived(ref, sem):
        pltpu.make_async_copy(ref, ref, sem).wait()

    def send_line(n):
        here = rz.at[z, :KC] if n == 0 else rz.at[z, KC:]
        for off in range(1, Z):
            remote(here, here, zs.at[n], zr.at[n], z_peer[off]).start()

    def line_arrived(n):
        ks = range(KC) if n == 0 else range(KC, NK)
        arrived(rz.at[: Z - 1, ks.start : ks.stop], zr.at[n])
        for zz in range(Z):
            for k in ks:
                line[k, zz * OWN : (zz + 1) * OWN, :] = rz[zz, k].astype(F32)
        full[c, ks.start : ks.stop, mine, :] = line[ks.start : ks.stop].astype(BF16)

    send_line(0)
    load_hole.wait()

    @pl.loop(0, AUX)
    def _(p):
        hole_t[pl.ds(pl.multiple_of(p * NO, NO), NO), :] = hole[p].T

    send_line(1)

    def spread(ch):
        here = full.at[c, pl.ds(ch * KC, KC), mine, :]
        for off in range(1, PLANE):
            remote(here, here, ps.at[ch], pr.at[ch], plane_peer[off]).start()

    def spread_done(ch):
        arrived(full.at[0, : KC * 2, : ROWS * (PLANE - 1) // 2], ps.at[ch])

    def hand_over(ch):
        arrived(full.at[0, : KC * 2, : ROWS * (PLANE - 1) // 2], pr.at[ch])
        for h in range(2):
            here = full.at[2 * h + core, pl.ds(ch * KC, KC)]
            remote(here, here, cs.at[ch], cr.at[ch], partner).start()

    def send_sums(ch):
        for off in range(1, LINES):
            rows = pl.ds(pl.multiple_of(line_at[off] * ROWS, ROWS), ROWS)
            remote(part.at[ch, rows, :], got.at[ch, ln], s1, r1.at[ch], line_peer[off]).start()

    def first_sum(ch):
        arrived(got.at[ch, : LINES - 1], r1.at[ch])
        total = got[ch, 0].astype(F32)
        for n in range(1, LINES):
            total = total + got[ch, n].astype(F32)
        for zz in range(Z):
            part2[ch, zz] = total[zz * OWN : (zz + 1) * OWN, :]
        got2[ch, z] = part2[ch, z]
        for off in range(1, Z):
            remote(part2.at[ch, z_at[off]], got2.at[ch, z], s2, r2.at[ch], z_peer[off]).start()

    def second_sum(ch):
        arrived(got2.at[ch, : Z - 1], r2.at[ch])
        total = got2[ch, 0]
        for n in range(1, Z):
            total = total + got2[ch, n]
        for kk in range(KC):
            k = ch * KC + kk
            out[k] = total[:, kk * W : (kk + 1) * W] + gap * rz[z, k].astype(F32)

    gap = jnp.concatenate([elec_e[...] - hole_e[i] for i in range(OWN)], axis=0)
    line_arrived(0)
    spread(0)
    line_arrived(1)
    load_elec.wait()
    spread_done(0)
    spread(1)
    hand_over(0)
    for ch in range(CH):
        arrived(full.at[:2, :KC], cr.at[ch])

        @pl.loop(0, AUX * W // MB)
        def _(m):
            left = elec[pl.ds(pl.multiple_of(m * MB, MB), MB), :]
            right = jnp.concatenate(
                [
                    jnp.concatenate([full[b, ch * KC + kk] for b in range(4)], axis=1)
                    for kk in range(KC)
                ],
                axis=0,
            )
            made = nt(left, right)
            for p in range(MB // W):
                at = pl.multiple_of(m * (MB // W * NO) + p * NO, NO)
                for kk in range(KC):
                    half[kk * W : (kk + 1) * W, pl.ds(at, NO)] = made[
                        p * W : (p + 1) * W, kk * NO : (kk + 1) * NO
                    ].astype(BF16)

            if ch + 2 < CH:
                @pl.when(m == 0)
                def _():
                    spread_done(ch + 1)
                    spread(ch + 2)

        if ch + 1 < CH:
            hand_over(ch + 1)
        if ch >= LAG:
            first_sum(ch - LAG)

        acc[...] = jnp.dot(half[...], hole_t[...], preferred_element_type=F32)
        part[ch] = acc[...].T.astype(BF16)
        got[ch, ln] = part[ch, mine, :]
        send_sums(ch)

        if ch >= LAG2:
            second_sum(ch - LAG2)

    for ch in range(CH - LAG, CH):
        first_sum(ch)
    for ch in range(CH - LAG2, CH):
        second_sum(ch)

    arrived(rz.at[: Z - 1, :KC], zs.at[0])
    arrived(rz.at[: Z - 1, KC:], zs.at[1])
    spread_done(CH - 1)
    for ch in range(CH):
        arrived(full.at[:2, :KC], cs.at[ch])
    arrived(got.at[:, : LINES - 1], s1)
    arrived(got2.at[:, : Z - 1], s2)


def local(trial, hole_factor, elec_factor, hole_energy, elec_energy):
    vmem, hbm = pl.BlockSpec(memory_space=pltpu.VMEM), pl.BlockSpec(memory_space=pl.ANY)
    dma = pltpu.SemaphoreType.DMA
    return pl.pallas_call(
        kernel,
        out_shape=jax.ShapeDtypeStruct((NK, OWN, W), F32),
        in_specs=[hbm, hbm, hbm, pl.BlockSpec(memory_space=pltpu.SMEM), vmem],
        out_specs=vmem,
        scratch_shapes=[
            pltpu.VMEM((AUX * W, NV), BF16),
            pltpu.VMEM((AUX, NO, NO), BF16),
            pltpu.VMEM((AUX * NO, NO), BF16),
            pltpu.VMEM((Z, NK, OWN, W), BF16),
            pltpu.VMEM((NK, ROWS, W), F32),
            pltpu.VMEM((4, NK, NO, W), BF16),
            pltpu.VMEM((KC * W, AUX * NO), BF16),
            pltpu.VMEM((KC * W, NO), F32),
            pltpu.VMEM((CH, NO, KC * W), BF16),
            pltpu.VMEM((CH, LINES, ROWS, KC * W), BF16),
            pltpu.VMEM((CH, Z, OWN, KC * W), F32),
            pltpu.VMEM((CH, Z, OWN, KC * W), F32),
            dma((3,)),
            dma((2,)), dma((2,)),
            dma((CH,)), dma((CH,)),
            dma((CH,)), dma((CH,)),
            dma, dma((CH,)),
            dma, dma((CH,)),
        ],
        compiler_params=pltpu.CompilerParams(
            collective_id=0, has_side_effects=True, vmem_limit_bytes=60 * 1024 * 1024
        ),
        name="bse_direct",
    )(
        trial, hole_factor, elec_factor.reshape(AUX * W, NV),
        hole_energy, elec_energy.reshape(1, W),
    )


def solution(mesh):
    in_specs = (
        P(None, "fit", "col"),
        P("fit", None, None),
        P("fit", "col", None),
        P("fit"),
        P("col"),
    )
    out_specs = P(None, "fit", "col")
    return jax.shard_map(local, mesh=mesh, in_specs=in_specs, out_specs=out_specs, check_vma=False)
```

time: 379 us -> 50.9 us (0.13)
  waiting for transfers between devices: 307 us -> 0 us
  Pallas kernels: 0 us -> 49.2 us
  matrix products: 24.8 us -> 0 us
  starting transfers between devices: 19.8 us -> 0 us
  between operations: 13.5 us -> 0.01 us
  blocking collectives: 8.82 us -> 0 us
    all_gather x1 -> x0, waiting for transfers between devices: 289 us -> none  [local(): lax.all_gather(wide_rows, 'fit', axis=1, tiled=True)]
    pallas_call x0 -> x1, Pallas kernels: none -> 49.2 us  [local(): pl.pallas_call(kernel, out_shape=jax.ShapeDtypeStruct((NK, OWN, W), F32),...]
    dot_general x1 -> x0, matrix products: 24.8 us -> none  [local(): jnp.einsum('pij,kpja->kia', hole_factor, half, preferred_element_type=jnp...]
    all_to_all x1 -> x0, starting transfers between devices: 19.8 us -> none  [summed_on_arrival(): lax.all_to_all(blocks, axis, split_axis=0, concat_axis=0, tiled=True)]
    all_to_all x1 -> x0, waiting for transfers between devices: 18.2 us -> none  [summed_on_arrival(): lax.all_to_all(blocks, axis, split_axis=0, concat_axis=0, tiled=True)]
    all_to_all x1 -> x0, blocking collectives: 8.82 us -> none  [copy_for_each(): lax.all_to_all(jnp.broadcast_to(array[None], (devices, *array.shape)), ax...]
  transfers between devices with their start and end apart: 2 -> 0, of which waited for: 2 -> 0; matrix products, arithmetic and copies ran while one was open for 0% -> 0% of each run, Pallas kernels for 0% -> 0%
where the time goes in v2:
time: 50.9 us; the launch traced here: 50.5 us
  Pallas kernels  49.2 us (97%)
  local copies, waits for them, and re-layouts  1.32 us (3%)
    pallas_call x1, Pallas kernels, local(): pl.pallas_call(kernel, out_shape=jax.ShapeDtypeStruct((NK, OWN, W), F32),...  49.2 us
    unnamed x1, local copies, waits for them, and re-layouts  1.32 us

profile of v2, /device:TPU:8, one launch (start us, length us, event | category | flops | bytes accessed | tf_op | source)
XLA Modules:
  0.0 50.5 jit_solution(18009599664887672072)
XLA Ops:
  0.0 49.2 %bse_direct.1 = f32[8,4,128]{2,1,0:T(4,128)} custom-call(bf16[8,4,128]{2,1,0:T(4,128)(2,1)} %trial.1, bf16[32,256,256]{2,1,0:T(8,128)(2,1)} %hole_hbm.1, bf16[4096,512]{1,0:T(8,128)(2,1)} %bitcast.2, f32[4]{0:T(128)} %hole_e.1, f32[1,128]{1,0:T(1,128)} %bitcast.3), custom_call_target="tpu_custom_call" | custom-call | tf_op jit(solution)/shard_map/bse_direct/pallas_call | solution.py:203
  49.2 1.3 %copy.7 = f32[8,4,128]{2,1,0:T(4,128)} copy(f32[8,4,128]{2,1,0:T(4,128)} %bse_direct.1) | data formatting | bytes 32768

commit v3 on v2

--- a/solution.py
+++ b/solution.py
@@ -27,8 +27,8 @@
 
 
 def kernel(
-    trial, hole_hbm, elec_hbm, hole_e, elec_e, out,
-    elec, hole, hole_t, rz, line, full, half, acc, part, got, part2, got2,
+    trial, hole_hbm, elec_hbm, hole_e_hbm, elec_e_hbm, out,
+    hole_e, elec_e, elec, hole, hole_t, rz, line, full, half, acc, part, got, part2, got2,
     load_sem, zs, zr, ps, pr, cs, cr, s1, r1, s2, r2,
 ):
     f, c = lax.axis_index("fit"), lax.axis_index("col")
@@ -56,6 +56,7 @@
     load_trial = load(0, trial, rz.at[z])
     load_hole = load(1, hole_hbm, hole)
     load_elec = load(2, elec_hbm, elec)
+    load_energies = [load(3, hole_e_hbm, hole_e), load(4, elec_e_hbm, elec_e)]
     load_trial.start()
 
     barrier = pltpu.get_barrier_semaphore()
@@ -63,6 +64,8 @@
         pl.semaphore_signal(barrier, inc=1, device_id=peer, device_id_type=MESH)
     load_hole.start()
     load_elec.start()
+    for one in load_energies:
+        one.start()
     load_trial.wait()
     pl.semaphore_wait(barrier, Z - 1 + PLANE - 1 + 1)
 
@@ -135,6 +138,8 @@
             k = ch * KC + kk
             out[k] = total[:, kk * W : (kk + 1) * W] + gap * rz[z, k].astype(F32)
 
+    for one in load_energies:
+        one.wait()
     gap = jnp.concatenate([elec_e[...] - hole_e[i] for i in range(OWN)], axis=0)
     line_arrived(0)
     spread(0)
@@ -142,6 +147,7 @@
     load_elec.wait()
     spread_done(0)
     spread(1)
+    spread(2)
     hand_over(0)
     for ch in range(CH):
         arrived(full.at[:2, :KC], cr.at[ch])
@@ -164,11 +170,11 @@
                         p * W : (p + 1) * W, kk * NO : (kk + 1) * NO
                     ].astype(BF16)
 
-            if ch + 2 < CH:
+            if ch == 0:
                 @pl.when(m == 0)
                 def _():
-                    spread_done(ch + 1)
-                    spread(ch + 2)
+                    spread_done(1)
+                    spread(3)
 
         if ch + 1 < CH:
             hand_over(ch + 1)
@@ -190,7 +196,8 @@
 
     arrived(rz.at[: Z - 1, :KC], zs.at[0])
     arrived(rz.at[: Z - 1, KC:], zs.at[1])
-    spread_done(CH - 1)
+    spread_done(2)
+    spread_done(3)
     for ch in range(CH):
         arrived(full.at[:2, :KC], cs.at[ch])
     arrived(got.at[:, : LINES - 1], s1)
@@ -198,14 +205,16 @@
 
 
 def local(trial, hole_factor, elec_factor, hole_energy, elec_energy):
-    vmem, hbm = pl.BlockSpec(memory_space=pltpu.VMEM), pl.BlockSpec(memory_space=pl.ANY)
+    vmem, hbm = pl.BlockSpec(memory_space=pltpu.VMEM), pl.BlockSpec(memory_space=pltpu.HBM)
     dma = pltpu.SemaphoreType.DMA
     return pl.pallas_call(
         kernel,
         out_shape=jax.ShapeDtypeStruct((NK, OWN, W), F32),
-        in_specs=[hbm, hbm, hbm, pl.BlockSpec(memory_space=pltpu.SMEM), vmem],
+        in_specs=[hbm] * 5,
         out_specs=vmem,
         scratch_shapes=[
+            pltpu.SMEM((OWN,), F32),
+            pltpu.VMEM((1, W), F32),
             pltpu.VMEM((AUX * W, NV), BF16),
             pltpu.VMEM((AUX, NO, NO), BF16),
             pltpu.VMEM((AUX * NO, NO), BF16),
@@ -218,7 +227,7 @@
             pltpu.VMEM((CH, LINES, ROWS, KC * W), BF16),
             pltpu.VMEM((CH, Z, OWN, KC * W), F32),
             pltpu.VMEM((CH, Z, OWN, KC * W), F32),
-            dma((3,)),
+            dma((5,)),
             dma((2,)), dma((2,)),
             dma((CH,)), dma((CH,)),
             dma((CH,)), dma((CH,)),

time: 50.9 us -> 48.6 us (0.955)
  Pallas kernels: 49.2 us -> 46.9 us
    pallas_call x1, Pallas kernels: 49.2 us -> 46.9 us  [local(): pl.pallas_call(kernel, out_shape=jax.ShapeDtypeStruct((NK, OWN, W), F32),...]
where the time goes in v3:
time: 48.6 us; the launch traced here: 48.3 us
  Pallas kernels  46.9 us (97%)
  local copies, waits for them, and re-layouts  1.32 us (3%)
    pallas_call x1, Pallas kernels, local(): pl.pallas_call(kernel, out_shape=jax.ShapeDtypeStruct((NK, OWN, W), F32),...  46.9 us
    unnamed x1, local copies, waits for them, and re-layouts  1.32 us

profile of v3, /device:TPU:8, one launch (start us, length us, event | category | flops | bytes accessed | tf_op | source)
XLA Modules:
  0.0 48.3 jit_solution(8196207608524934730)
XLA Ops:
  0.0 46.9 %bse_direct.1 = f32[8,4,128]{2,1,0:T(4,128)} custom-call(bf16[8,4,128]{2,1,0:T(4,128)(2,1)} %trial.1, bf16[32,256,256]{2,1,0:T(8,128)(2,1)} %hole_hbm.1, bf16[4096,512]{1,0:T(8,128)(2,1)} %bitcast.2, f32[4]{0:T(128)} %hole_e_hbm.1, f32[1,128]{1,0:T(1,128)} %bitcast.3), custom_call_target="tpu_custom_call" | custom-call | tf_op jit(solution)/shard_map/bse_direct/pallas_call | solution.py:210
  46.9 1.3 %copy.7 = f32[8,4,128]{2,1,0:T(4,128)} copy(f32[8,4,128]{2,1,0:T(4,128)} %bse_direct.1) | data formatting | bytes 32768

commit v4 on v3

--- a/solution.py
+++ b/solution.py
@@ -147,8 +147,8 @@
     load_elec.wait()
     spread_done(0)
     spread(1)
+    hand_over(0)
     spread(2)
-    hand_over(0)
     for ch in range(CH):
         arrived(full.at[:2, :KC], cr.at[ch])
 
@@ -173,7 +173,6 @@
             if ch == 0:
                 @pl.when(m == 0)
                 def _():
-                    spread_done(1)
                     spread(3)
 
         if ch + 1 < CH:
@@ -196,8 +195,8 @@
 
     arrived(rz.at[: Z - 1, :KC], zs.at[0])
     arrived(rz.at[: Z - 1, KC:], zs.at[1])
-    spread_done(2)
-    spread_done(3)
+    for ch in range(1, CH):
+        spread_done(ch)
     for ch in range(CH):
         arrived(full.at[:2, :KC], cs.at[ch])
     arrived(got.at[:, : LINES - 1], s1)

time: 48.6 us -> 48.7 us (level)
  no operation moved by 1% of the time
where the time goes in v4:
time: 48.7 us; the launch traced here: 47.9 us
  Pallas kernels  46.6 us (96%)
  local copies, waits for them, and re-layouts  1.32 us (3%)
    pallas_call x1, Pallas kernels, local(): pl.pallas_call(kernel, out_shape=jax.ShapeDtypeStruct((NK, OWN, W), F32),...  46.6 us
    unnamed x1, local copies, waits for them, and re-layouts  1.32 us

profile of v4, /device:TPU:8, one launch (start us, length us, event | category | flops | bytes accessed | tf_op | source)
XLA Modules:
  0.0 47.9 jit_solution(10347793235380262852)
XLA Ops:
  0.0 46.6 %bse_direct.1 = f32[8,4,128]{2,1,0:T(4,128)} custom-call(bf16[8,4,128]{2,1,0:T(4,128)(2,1)} %trial.1, bf16[32,256,256]{2,1,0:T(8,128)(2,1)} %hole_hbm.1, bf16[4096,512]{1,0:T(8,128)(2,1)} %bitcast.2, f32[4]{0:T(128)} %hole_e_hbm.1, f32[1,128]{1,0:T(1,128)} %bitcast.3), custom_call_target="tpu_custom_call" | custom-call | tf_op jit(solution)/shard_map/bse_direct/pallas_call | solution.py:209
  46.6 1.3 %copy.7 = f32[8,4,128]{2,1,0:T(4,128)} copy(f32[8,4,128]{2,1,0:T(4,128)} %bse_direct.1) | data formatting | bytes 32768
